TPU v7x, 256 devices: a whole 4x4x8 slice. The times are simulated.
256 devices in a mesh: dp: 32 (over y, x, core), mp: 8 (over z).
Axes of the slice: x: 4, y: 4, z: 8, core: 2. Of those that a mesh axis runs over, the one named last changes fastest.
Arguments:
- clean: bfloat16 [128, 256, 1536], P('dp', None, 'mp'), may hold values from -6 to 6
- noise: bfloat16 [128, 256, 1536], P('dp', None, 'mp'), may hold values from -6 to 6
- teacher_first: bfloat16 [128, 256, 1536], P('dp', None, 'mp'), may hold values from -6 to 6
- teacher_second: bfloat16 [128, 256, 1536], P('dp', None, 'mp'), may hold values from -6 to 6
- step_index: int32 [128], P('dp'), may hold values from 8 to 32
- teacher_count: int32 [128], P('dp'), may hold values from 64 to 256
- up_master: float32 [1536, 6144], P('dp', 'mp'), may hold values from -6 to 6
- down_master: float32 [1536, 6144], P('dp', 'mp'), may hold values from -6 to 6
- up_moment: float32 [1536, 6144], P('dp', 'mp'), may hold values from -1.8 to 1.8
- down_moment: float32 [1536, 6144], P('dp', 'mp'), may hold values from -1.8 to 1.8
- up_second: float32 [1536, 6144], P('dp', 'mp'), may hold values from 0.002 to 0.032
- down_second: float32 [1536, 6144], P('dp', 'mp'), may hold values from 0.002 to 0.032
Outputs:
- new_up_master: float32 [1536, 6144], P('dp', 'mp')
- new_down_master: float32 [1536, 6144], P('dp', 'mp')
- new_up_moment: float32 [1536, 6144], P('dp', 'mp')
- new_down_moment: float32 [1536, 6144], P('dp', 'mp')
- new_up_second: float32 [1536, 6144], P('dp', 'mp')
- new_down_second: float32 [1536, 6144], P('dp', 'mp')
- loss_mean: float32 [], replicated
Inputs may be any that keep to these rules, and one draw needn't show every extreme that they name: `step_index`: student step k with 2k at most the sample's teacher_count.
All inputs are finite; a program needn't handle non-finite values.
Results may differ from a plain program's by a relative error of at most 0.002.
Values may be sent and summed in bfloat16 or wider, within the bound.
No kernel may reach another device: no remote copies, remote signals or barrier semaphores. Data moves between devices by JAX's collectives and lax.ppermute only.
A program may use at most 64 MiB of HBM per device.

v0:
```python
import functools
import math
import jax
import jax.numpy as jnp
from jax import lax
from jax.sharding import Mesh
from jax.sharding import PartitionSpec as P

DP = ("dp_0", "dp_1", "dp_2")
DP_MP = ("dp_0", "dp_1", "dp_2", "mp")
adam_count = 100.0
learn_rate = 0.05
decay_rate = 0.01


def sent_together(arrays, axis, dim, along):
    both = jnp.concatenate(arrays, axis=along)
    result, at, outs = (lax.all_gather(both, axis, axis=dim, tiled=True), 0, [])
    for a in arrays:
        outs.append(lax.slice_in_dim(result, at, at + a.shape[along], axis=along))
        at += a.shape[along]
    return tuple(outs)


def sent_together_2(arrays, axis, dim, along):
    ends, at = ([], 0)
    for a in arrays[:-1]:
        at += a.shape[along]
        ends.append(at)
    both = jnp.concatenate(arrays, axis=along)
    return tuple(
        jnp.split(lax.psum_scatter(both, axis, scatter_dimension=dim, tiled=True), ends, axis=along)
    )


def by_axis(shard, axes):
    return functools.reduce(lax.psum, axes, shard)


def gelu_pair(preact):
    tanh_arg = 0.7978845608028654 * (preact + 0.044715 * preact * preact * preact)
    tanh_val = jnp.tanh(tanh_arg)
    activation = 0.5 * preact * (1.0 + tanh_val)
    slopes = 0.5 * (1.0 + tanh_val) + 0.5 * preact * (
        1.0 - tanh_val * tanh_val
    ) * 0.7978845608028654 * (1.0 + 3.0 * 0.044715 * preact * preact)
    return (activation, slopes)


def distill_target(clean, noise, teacher_first, teacher_second, step_index, teacher_count):
    steps_float = teacher_count.astype(jnp.float32)[:, None, None]
    doubled = 2.0 * step_index.astype(jnp.float32)[:, None, None]
    quarter_turn = 0.5 * math.pi
    time_now = doubled / steps_float
    time_mid = (doubled - 1.0) / steps_float
    time_end = (doubled - 2.0) / steps_float
    alpha_now = jnp.cos(quarter_turn * time_now)
    sigma_now = jnp.sin(quarter_turn * time_now)
    alpha_mid = jnp.cos(quarter_turn * time_mid)
    sigma_mid = jnp.sin(quarter_turn * time_mid)
    alpha_end = jnp.cos(quarter_turn * time_end)
    sigma_end = jnp.sin(quarter_turn * time_end)
    first_f = teacher_first.astype(jnp.float32)
    second_f = teacher_second.astype(jnp.float32)
    latent_now = alpha_now * clean.astype(jnp.float32) + sigma_now * noise.astype(jnp.float32)
    noise_now = (latent_now - alpha_now * first_f) / sigma_now
    latent_mid = alpha_mid * first_f + sigma_mid * noise_now
    noise_mid = (latent_mid - alpha_mid * second_f) / sigma_mid
    latent_end = alpha_end * second_f + sigma_end * noise_mid
    sigma_ratio = sigma_end / sigma_now
    target = (latent_end - sigma_ratio * latent_now) / (alpha_end - sigma_ratio * alpha_now)
    weighting = jnp.maximum(alpha_now * alpha_now / (sigma_now * sigma_now), 1.0)[:, 0, 0]
    return (latent_now, target, weighting)


def adam_update(master, moment, second, gradient, factor):
    clipped = gradient * factor
    moment_new = 0.9 * moment + 0.1 * clipped
    second_new = 0.999 * second + 0.001 * clipped * clipped
    first_hat = moment_new / (1.0 - 0.9**adam_count)
    second_hat = second_new / (1.0 - 0.999**adam_count)
    master_new = master - learn_rate * (
        first_hat / (jnp.sqrt(second_hat) + 1e-08) + decay_rate * master
    )
    return (master_new, moment_new, second_new)


def per_device(
    clean,
    noise,
    teacher_first,
    teacher_second,
    step_index,
    teacher_count,
    up_master,
    down_master,
    up_moment,
    down_moment,
    up_second,
    down_second,
):
    samples_dev, token_count, width_local = clean.shape
    sample_total = samples_dev * lax.axis_size(DP)
    row_count = samples_dev * token_count
    latent, target, weighting = distill_target(
        clean, noise, teacher_first, teacher_second, step_index, teacher_count
    )
    noisy_rows = latent.reshape(row_count, width_local).astype(jnp.bfloat16)
    gathered = lax.all_gather(noisy_rows, "mp", axis=1, tiled=True)
    gathered_f = gathered.astype(jnp.float32)
    normed = (
        gathered_f * lax.rsqrt(jnp.mean(gathered_f * gathered_f, axis=1, keepdims=True) + 1e-06)
    ).astype(jnp.bfloat16)
    up_full, down_full = sent_together(
        (up_master.astype(jnp.bfloat16), down_master.astype(jnp.bfloat16)), DP, 0, 1
    )
    width_full = up_full.shape[0]
    hidden_local = up_full.shape[1]
    dscale = width_full ** (-0.5)
    fscale = (hidden_local * lax.axis_size("mp")) ** (-0.5)
    preact = jnp.dot(normed, up_full, preferred_element_type=jnp.float32) * dscale
    activation, slopes = gelu_pair(preact)
    hidden = activation.astype(jnp.bfloat16)
    partial_value = (
        lax.dot_general(
            hidden, down_full, (((1,), (1,)), ((), ())), preferred_element_type=jnp.float32
        )
        * fscale
    )
    branch = lax.psum_scatter(
        partial_value.astype(jnp.bfloat16), "mp", scatter_dimension=1, tiled=True
    ).astype(jnp.float32)
    errors = latent + branch.reshape(latent.shape) - target
    weight_cube = weighting[:, None, None]
    loss_part = jnp.sum(weight_cube * errors * errors)
    dpred = (
        (2.0 * weight_cube / sample_total * errors)
        .astype(jnp.bfloat16)
        .reshape(row_count, width_local)
    )
    piece = lax.all_gather(dpred, "mp", axis=1, tiled=True)
    summed = jnp.dot(piece, down_full, preferred_element_type=jnp.float32)
    grad_piece = (
        lax.dot_general(piece, hidden, (((0,), (0,)), ((), ())), preferred_element_type=jnp.float32)
        * fscale
    )
    dpre = (summed * fscale * slopes).astype(jnp.bfloat16)
    grad_up = (
        lax.dot_general(normed, dpre, (((0,), (0,)), ((), ())), preferred_element_type=jnp.float32)
        * dscale
    )
    owned_up, owned_down = sent_together_2((grad_up, grad_piece), DP, 0, 1)
    squares = jnp.sum(owned_up * owned_up) + jnp.sum(owned_down * owned_down)
    loss_total, square_total = (by_axis(loss_part, DP_MP), by_axis(squares, DP_MP))
    clip_limit = math.sqrt(2.0 * width_full * hidden_local * lax.axis_size("mp"))
    factor = clip_limit / jnp.maximum(jnp.sqrt(square_total), clip_limit)
    new_up, up_m, up_v = adam_update(up_master, up_moment, up_second, owned_up, factor)
    new_down, down_m, down_v = adam_update(
        down_master, down_moment, down_second, owned_down, factor
    )
    loss_mean = loss_total / (sample_total * token_count * width_full)
    return (new_up, new_down, up_m, down_m, up_v, down_v, loss_mean)


def solution(mesh):
    split = Mesh(mesh.devices.reshape(4, 4, 2, mesh.shape["mp"]), ("dp_0", "dp_1", "dp_2", "mp"))
    placed = (
        P(DP, None, "mp"),
        P(DP, None, "mp"),
        P(DP, None, "mp"),
        P(DP, None, "mp"),
        P(DP),
        P(DP),
        P(DP, "mp"),
        P(DP, "mp"),
        P(DP, "mp"),
        P(DP, "mp"),
        P(DP, "mp"),
        P(DP, "mp"),
    )
    return jax.shard_map(
        per_device,
        mesh=split,
        in_specs=placed,
        out_specs=(
            P(DP, "mp"),
            P(DP, "mp"),
            P(DP, "mp"),
            P(DP, "mp"),
            P(DP, "mp"),
            P(DP, "mp"),
            P(),
        ),
        check_vma=False,
    )
```

profile of v0, /device:TPU:2, one launch (start us, length us, event | category | flops | bytes accessed | tf_op | source)
XLA Modules:
  0.0 404.3 jit_solution(1169654670336712328)
XLA Ops:
  7.2 0.7 fusion.39
  8.0 1.3 fusion.27
  9.3 0.8 copy.76
  10.2 0.9 convert_element_type.57
  11.2 0.9 convert_element_type.58
  12.1 0.7 pad_maximum_fusion.1
  12.8 0.0 reduce-scatter.5.cloned.1.call-start
  12.8 45.4 %all-gather.4.cloned.1.call-done = bf16[1024,1536]{0,1:T(8,128)(2,1)} async-done(((bf16[1024,192]{0,1:T(8,128)(2,1)}), bf16[1024,1536]{0,1:T(8,128)(2,1)}) %all-gather.4.cloned.1.call-update) | async-done | bytes 3145744 | tf_op jit(solution)/shard_map/all_gather | solution.py:109
  58.3 2.7 fusion
  61.0 50.3 %all-gather.6.cloned.1.call-done = bf16[1536,1536]{1,0:T(8,128)(2,1)} async-done(((bf16[48,1536]{1,0:T(8,128)(2,1)}), bf16[1536,1536]{1,0:T(8,128)(2,1)}) %all-gather.6.cloned.1.call-update) | async-done | bytes 4718608 | tf_op jit(solution)/shard_map/all_gather | solution.py:18
  111.3 4.6 %fusion.6 = f32[1024,768]{1,0:T(8,128)S(1)} fusion(bf16[1024,1536]{0,1:T(8,128)(2,1)S(1)} %copy-done, f32[1024]{0:T(1024)S(1)} %add_rsqrt_fusion, bf16[1536,1536]{1,0:T(8,128)(2,1)} %all-gather.6.cloned.1.call-done), kind=kOutput, calls=%fused_computation.14 | convolution fusion | flops 2420637696 | bytes 8654848 | tf_op jit(solution)/shard_map/dot_general | solution.py:121
  115.9 1.8 copy-done.14
  117.7 4.4 %multiply_convert_fusion = bf16[1024,1536]{0,1:T(8,128)(2,1)} fusion(bf16[1536,1536]{1,0:T(8,128)(2,1)S(1)} %copy-done.12, f32[1024,768]{1,0:T(8,128)S(1)} %fusion.6), kind=kOutput, calls=%fused_computation.5 | convolution fusion | flops 2426929152 | bytes 8650752 | tf_op jit(solution)/shard_map/dot_general | solution.py:125
  122.2 46.7 %reduce-scatter.5.cloned.1.call-done = bf16[1024,192]{0,1:T(8,128)(2,1)} async-done(((bf16[1024,1536]{0,1:T(8,128)(2,1)}), bf16[1024,192]{0,1:T(8,128)(2,1)}) %reduce-scatter.5.cloned.1.call-update) | async-done | bytes 393232 | tf_op jit(solution)/shard_map/reduce_scatter | solution.py:130
  169.0 1.1 reshape.70
  170.1 1.5 fusion.25
  171.6 0.1 fusion.28
  171.7 0.8 copy.77
  172.5 0.2 reduce-scatter.7.cloned.1.call-start
  172.8 44.4 %all-gather.8.cloned.1.call-done = bf16[1024,1536]{0,1:T(8,128)(2,1)} async-done(((bf16[1024,192]{0,1:T(8,128)(2,1)}), bf16[1024,1536]{0,1:T(8,128)(2,1)}) %all-gather.8.cloned.1.call-update) | async-done | bytes 3145744 | tf_op jit(solution)/shard_map/all_gather | solution.py:141
  217.2 8.1 %multiply_convert_fusion.1 = bf16[1024,768]{1,0:T(8,128)(2,1)S(1)} fusion(f32[1024,768]{1,0:T(8,128)} %copy-done.14, bf16[1024,1536]{0,1:T(8,128)(2,1)} %all-gather.8.cloned.1.call-done, bf16[1536,1536]{1,0:T(8,128)(2,1)} %all-gather.6.cloned.1.call-done), kind=kOutput, calls=%fused_computation.11 | convolution fusion | flops 2432434176 | bytes 10223616 | tf_op jit(solution)/shard_map/dot_general | solution.py:142
  225.3 5.2 %convolution_multiply_fusion = f32[1536,768]{0,1:T(8,128)S(1)} fusion(bf16[1024,1536]{0,1:T(8,128)(2,1)S(1)} %copy-done.13, f32[1024,768]{1,0:T(8,128)} %copy-done.14), kind=kOutput, calls=%fused_computation.7 | convolution fusion | flops 2424963072 | bytes 11010048 | tf_op jit(solution)/shard_map/dot_general | solution.py:144
  230.5 2.8 convolution_multiply_fusion.1
  233.3 4.5 %pad_maximum_fusion = f32[1536,1536]{0,1:T(8,128)} fusion(f32[1536,768]{0,1:T(8,128)S(1)} %convolution_multiply_fusion, f32[1536,768]{0,1:T(8,128)S(1)} %convolution_multiply_fusion.1), kind=kLoop, calls=%fused_computation | loop fusion | flops 2359296 | bytes 18874368 | tf_op jit(solution)/shard_map/concatenate | solution.py:30
  237.8 9.6 %copy.73 = f32[1536,1536]{1,0:T(8,128)} copy(f32[1536,1536]{0,1:T(8,128)} %pad_maximum_fusion) | data formatting | bytes 18874368
  247.5 101.6 %reduce-scatter.7.cloned.1.call-done = f32[48,1536]{1,0:T(8,128)} async-done(((f32[1536,1536]{1,0:T(8,128)}), f32[48,1536]{1,0:T(8,128)}) %reduce-scatter.7.cloned.1.call-update) | async-done | bytes 294928 | tf_op jit(solution)/shard_map/reduce_scatter | solution.py:32
  349.1 1.6 multiply_reduce_fusion
  352.0 9.9 %all-reduce.2 = (f32[]{:T(128)}, f32[]{:T(128)}) all-reduce(f32[]{:T(128)S(6)} %add.97, f32[]{:T(128)} %get-tuple-element.44), channel_id=1, replica_groups=mesh['dp_0'=4,'dp_1'=4,'dp_2'=2,'mp'=8] {'dp_0'}, use_global_device_ids=true, to_apply=%region_5.0 | all-reduce | flops 2 | bytes 16 | tf_op jit(solution)/shard_map/psum | solution.py:37
  361.9 10.1 %all-reduce.1 = (f32[]{:T(128)}, f32[]{:T(128)}) all-reduce(f32[]{:T(128)} %get-tuple-element.34, f32[]{:T(128)} %get-tuple-element.35), channel_id=1, replica_groups=mesh['dp_0'=4,'dp_1'=4,'dp_2'=2,'mp'=8] {'dp_1'}, use_global_device_ids=true, to_apply=%region_6.0 | all-reduce | flops 2 | bytes 16 | tf_op jit(solution)/shard_map/psum | solution.py:37
  372.0 3.1 all-reduce.3
  375.1 18.1 %all-reduce = (f32[]{:T(128)}, f32[]{:T(128)}) all-reduce(f32[]{:T(128)} %get-tuple-element.36, f32[]{:T(128)} %get-tuple-element.37), channel_id=1, replica_groups=mesh['dp_0'=4,'dp_1'=4,'dp_2'=2,'mp'=8] {'mp'}, use_global_device_ids=true, to_apply=%region_8.0 | all-reduce | flops 2 | bytes 16 | tf_op jit(solution)/shard_map/psum | solution.py:37
  394.6 2.0 multiply_subtract_fusion
  (42 shorter events, 0.4 us)
Async XLA Ops:
  7.2 51.1 %all-gather.4.cloned.1.call-start = ((), (), s32[]{:S(2)}) async-start(), calls=%async_computation.2 | async-start | bytes 3538944 | tf_op jit(solution)/shard_map/all_gather | solution.py:109
  10.2 101.2 %all-gather.6.cloned.1.call-start = ((), (), s32[]{:S(2)}) async-start(), calls=%async_computation.3 | async-start | bytes 4866048 | tf_op jit(solution)/shard_map/all_gather | solution.py:18
  12.8 156.2 %reduce-scatter.5.cloned.1.call-start = ((), (), s32[]{:S(2)}) async-start(), calls=%async_computation.4 | async-start | bytes 3538944 | tf_op jit(solution)/shard_map/reduce_scatter | solution.py:130
  58.3 53.1 %copy-start = (bf16[1024,1536]{0,1:T(8,128)(2,1)S(1)}, bf16[1024,1536]{0,1:T(8,128)(2,1)}, u32[]{:S(2)}) copy-start(bf16[1024,1536]{0,1:T(8,128)(2,1)} %all-gather.4.cloned.1.call-done) | copy-start | bytes 9437188
  111.3 6.4 %copy-start.12 = (bf16[1536,1536]{1,0:T(8,128)(2,1)S(1)}, bf16[1536,1536]{1,0:T(8,128)(2,1)}, u32[]{:S(2)}) copy-start(bf16[1536,1536]{1,0:T(8,128)(2,1)} %all-gather.6.cloned.1.call-done) | copy-start | bytes 14155780
  115.9 1.8 copy-start.14
  122.1 48.0 %copy-start.2 = (bf16[4,256,192]{1,2,0:T(8,128)(2,1)S(1)}, bf16[4,256,192]{1,2,0:T(8,128)(2,1)}, u32[]{:S(2)}) copy-start(bf16[4,256,192]{1,2,0:T(8,128)(2,1)} %param.13) | copy-start | bytes 1179652
  122.1 48.0 %copy-start.3 = (bf16[4,256,192]{1,2,0:T(8,128)(2,1)S(1)}, bf16[4,256,192]{1,2,0:T(8,128)(2,1)}, u32[]{:S(2)}) copy-start(bf16[4,256,192]{1,2,0:T(8,128)(2,1)} %param.12) | copy-start | bytes 1179652
  122.1 48.0 %copy-start.6 = (bf16[4,256,192]{1,2,0:T(8,128)(2,1)S(1)}, bf16[4,256,192]{1,2,0:T(8,128)(2,1)}, u32[]{:S(2)}) copy-start(bf16[4,256,192]{1,2,0:T(8,128)(2,1)} %param.14) | copy-start | bytes 1179652
  122.1 48.0 %copy-start.7 = (bf16[4,256,192]{1,2,0:T(8,128)(2,1)S(1)}, bf16[4,256,192]{1,2,0:T(8,128)(2,1)}, u32[]{:S(2)}) copy-start(bf16[4,256,192]{1,2,0:T(8,128)(2,1)} %param.15) | copy-start | bytes 1179652
  122.1 95.1 %all-gather.8.cloned.1.call-start = ((), (), s32[]{:S(2)}) async-start(), calls=%async_computation.5 | async-start | bytes 3538944 | tf_op jit(solution)/shard_map/all_gather | solution.py:141
  172.5 176.6 %reduce-scatter.7.cloned.1.call-start = ((), (), s32[]{:S(2)}) async-start(), calls=%async_computation.6 | async-start | bytes 9732096 | tf_op jit(solution)/shard_map/reduce_scatter | solution.py:32
  217.2 8.1 %copy-start.13 = (bf16[1024,1536]{0,1:T(8,128)(2,1)S(1)}, bf16[1024,1536]{0,1:T(8,128)(2,1)}, u32[]{:S(2)}) copy-start(bf16[1024,1536]{0,1:T(8,128)(2,1)} %all-gather.8.cloned.1.call-done) | copy-start | bytes 9437188
  225.3 5.2 %copy-start.1 = (bf16[1024,1536]{0,1:T(8,128)(2,1)S(1)}, bf16[1024,1536]{0,1:T(8,128)(2,1)}, u32[]{:S(2)}) copy-start(bf16[1024,1536]{0,1:T(8,128)(2,1)} %all-gather.4.cloned.1.call-done) | copy-start | bytes 9437188
  247.5 147.1 %copy-start.4 = (f32[48,768]{1,0:T(8,128)S(1)}, f32[48,768]{1,0:T(8,128)}, u32[]{:S(2)}) copy-start(f32[48,768]{1,0:T(8,128)} %param.19) | copy-start | bytes 442372
  247.5 147.1 %copy-start.5 = (f32[48,768]{1,0:T(8,128)S(1)}, f32[48,768]{1,0:T(8,128)}, u32[]{:S(2)}) copy-start(f32[48,768]{1,0:T(8,128)} %param.18) | copy-start | bytes 442372
  247.5 147.1 %copy-start.8 = (f32[48,768]{1,0:T(8,128)S(1)}, f32[48,768]{1,0:T(8,128)}, u32[]{:S(2)}) copy-start(f32[48,768]{1,0:T(8,128)} %param.21) | copy-start | bytes 442372
  247.5 147.1 %copy-start.9 = (f32[48,768]{1,0:T(8,128)S(1)}, f32[48,768]{1,0:T(8,128)}, u32[]{:S(2)}) copy-start(f32[48,768]{1,0:T(8,128)} %param.23) | copy-start | bytes 442372
  247.5 147.1 %copy-start.10 = (f32[48,768]{1,0:T(8,128)S(1)}, f32[48,768]{1,0:T(8,128)}, u32[]{:S(2)}) copy-start(f32[48,768]{1,0:T(8,128)} %param.22) | copy-start | bytes 442372
  247.5 147.1 %copy-start.11 = (f32[48,768]{1,0:T(8,128)S(1)}, f32[48,768]{1,0:T(8,128)}, u32[]{:S(2)}) copy-start(f32[48,768]{1,0:T(8,128)} %param.20) | copy-start | bytes 442372
Sparse Core Ops, SparseCore 0:
  10.3 47.9 all-gather.3
  61.4 49.9 all-gather.5
  122.2 46.7 reduce-scatter.4
  172.6 44.4 all-gather.7
  247.6 101.4 reduce-scatter.6
where the time goes:
time: 405 us; the launch traced here: 404 us
  waiting for transfers between devices  289 us (71%)
  blocking collectives  41.1 us (10%)
  matrix products  25 us (6%)
  other arithmetic  18.2 us (4%)
  between operations  17.8 us (4%)
  local copies, waits for them, and re-layouts  13.2 us (3%)
    reduce_scatter x1, waiting for transfers between devices, sent_together_2(): lax.psum_scatter(both, axis, scatter_dimension=dim, tiled=True)  102 us
    all_gather x1, waiting for transfers between devices, sent_together(): result, at, outs = (lax.all_gather(both, axis, axis=dim, tiled=True), 0, [])  50.3 us
    reduce_scatter x1, waiting for transfers between devices, per_device(): lax.psum_scatter(partial_value.astype(jnp.bfloat16), 'mp', scatter_dimens...  46.7 us
    all_gather x1, waiting for transfers between devices, per_device(): gathered = lax.all_gather(noisy_rows, 'mp', axis=1, tiled=True)  45.4 us
    all_gather x1, waiting for transfers between devices, per_device(): piece = lax.all_gather(dpred, 'mp', axis=1, tiled=True)  44.4 us
    psum x4, blocking collectives, by_axis(): return functools.reduce(lax.psum, axes, shard)  41.1 us
    unnamed x31, local copies, waits for them, and re-layouts  11.5 us
  transfers between devices with their start and end apart: 5, of which 5 were waited for; matrix products, arithmetic and copies ran while one was open for 1% of the time, Pallas kernels for 0%

commit v1 on v0

--- a/solution.py
+++ b/solution.py
@@ -5,6 +5,7 @@
 from jax import lax
 from jax.sharding import Mesh
 from jax.sharding import PartitionSpec as P
+from jax.lax import all_to_all, axis_size
 
 DP = ("dp_0", "dp_1", "dp_2")
 DP_MP = ("dp_0", "dp_1", "dp_2", "mp")
@@ -106,7 +107,9 @@
         clean, noise, teacher_first, teacher_second, step_index, teacher_count
     )
     noisy_rows = latent.reshape(row_count, width_local).astype(jnp.bfloat16)
-    gathered = lax.all_gather(noisy_rows, "mp", axis=1, tiled=True)
+    a_now = jnp.stack([noisy_rows for _ in range(axis_size("mp"))])
+    carry_out = all_to_all(a_now, "mp", 0, 0)
+    gathered = jnp.concatenate(carry_out, axis=1)
     gathered_f = gathered.astype(jnp.float32)
     normed = (
         gathered_f * lax.rsqrt(jnp.mean(gathered_f * gathered_f, axis=1, keepdims=True) + 1e-06)

time: 405 us -> 385 us (0.951)
  waiting for transfers between devices: 289 us -> 187 us
  blocking collectives: 41.1 us -> 123 us
    all_to_all x0 -> x1, blocking collectives: none -> 81.9 us  [per_device(): carry_out = all_to_all(a_now, 'mp', 0, 0)]
    all_gather x1, waiting for transfers between devices: 50.3 us -> 0.02 us  [sent_together(): result, at, outs = (lax.all_gather(both, axis, axis=dim, tiled=True), 0, [])]
    all_gather x1 -> x0, waiting for transfers between devices: 45.4 us -> none  [per_device(): gathered = lax.all_gather(noisy_rows, 'mp', axis=1, tiled=True)]
    reduce_scatter x1, waiting for transfers between devices: 46.7 us -> 41 us  [per_device(): lax.psum_scatter(partial_value.astype(jnp.bfloat16), 'mp', scatter_dimens...]
    unnamed x31 -> x27, local copies, waits for them, and re-layouts: 11.5 us -> 11.3 us
  transfers between devices with their start and end apart: 5 -> 4, of which waited for: 5 -> 3; matrix products, arithmetic and copies ran while one was open for 1% -> 2% of each run, Pallas kernels for 0% -> 0%
where the time goes in v1:
time: 385 us
  waiting for transfers between devices  187 us (49%)
  blocking collectives  123 us (32%)
  matrix products  22.9 us (6%)
  other arithmetic  19.3 us (5%)
  between operations  17.8 us (5%)
  local copies, waits for them, and re-layouts  14.6 us (4%)
    reduce_scatter x1, waiting for transfers between devices, sent_together_2(): lax.psum_scatter(both, axis, scatter_dimension=dim, tiled=True)  102 us
    all_to_all x1, blocking collectives, per_device(): carry_out = all_to_all(a_now, 'mp', 0, 0)  81.9 us
    all_gather x1, waiting for transfers between devices, per_device(): piece = lax.all_gather(dpred, 'mp', axis=1, tiled=True)  44.4 us
    psum x4, blocking collectives, by_axis(): return functools.reduce(lax.psum, axes, shard)  41.1 us
    reduce_scatter x1, waiting for transfers between devices, per_device(): lax.psum_scatter(partial_value.astype(jnp.bfloat16), 'mp', scatter_dimens...  41 us
    unnamed x27, local copies, waits for them, and re-layouts  11.3 us
    dot_general x1, matrix products, per_device(): summed = jnp.dot(piece, down_full, preferred_element_type=jnp.float32)  7.96 us
  transfers between devices with their start and end apart: 4, of which 3 were waited for; matrix products, arithmetic and copies ran while one was open for 2% of the time, Pallas kernels for 0%

profile of v1, /device:TPU:2, one launch (start us, length us, event | category | flops | bytes accessed | tf_op | source)
XLA Modules:
  0.0 384.9 jit_solution(5067227110878487639)
XLA Ops:
  7.2 0.9 convert_element_type.72
  8.1 0.9 convert_element_type.73
  9.1 0.7 pad_maximum_fusion.1
  9.8 1.2 fusion.36
  11.1 1.3 fusion.24
  12.4 0.4 stack.2
  12.8 81.9 %all_to_all.5 = bf16[8,1024,192]{1,2,0:T(8,128)(2,1)S(1)} all-to-all(bf16[8,1024,192]{1,2,0:T(8,128)(2,1)S(1)} %stack.2), channel_id=1, replica_groups=mesh['dp_0'=4,'dp_1'=4,'dp_2'=2,'mp'=8] {'mp'}, dimensions={0} | all-to-all | bytes 6291456 | tf_op jit(solution)/shard_map/all_to_all | solution.py:111
  94.8 0.7 multiply_reduce_fusion
  95.5 0.9 fusion
  96.4 4.6 %fusion.4 = f32[1024,768]{1,0:T(8,128)S(1)} fusion(bf16[1024,1536]{0,1:T(8,128)(2,1)S(1)} %fusion, bf16[1536,1536]{1,0:T(8,128)(2,1)} %all-gather.3.cloned.1.call-done), kind=kOutput, calls=%fused_computation.13 | convolution fusion | flops 2415919104 | bytes 8650752 | tf_op jit(solution)/shard_map/dot_general | solution.py:124
  101.0 1.6 copy-done.11
  102.7 4.5 %multiply_convert_fusion = bf16[1024,1536]{0,1:T(8,128)(2,1)} fusion(bf16[1536,1536]{1,0:T(8,128)(2,1)S(1)} %copy-done.9, f32[1024,768]{1,0:T(8,128)S(1)} %fusion.4), kind=kOutput, calls=%fused_computation.3 | convolution fusion | flops 2426929152 | bytes 8650752 | tf_op jit(solution)/shard_map/dot_general | solution.py:128
  107.2 0.7 cos.13
  108.0 1.2 sin.14
  109.2 0.5 multiply_subtract_fusion.2
  109.7 41.0 %reduce-scatter.5.cloned.1.call-done = bf16[1024,192]{0,1:T(8,128)(2,1)} async-done(((bf16[1024,1536]{0,1:T(8,128)(2,1)}), bf16[1024,192]{0,1:T(8,128)(2,1)}) %reduce-scatter.5.cloned.1.call-update) | async-done | bytes 393232 | tf_op jit(solution)/shard_map/reduce_scatter | solution.py:133
  150.7 1.1 reshape.78
  151.8 2.7 fusion.22
  154.7 0.8 copy.77
  155.7 44.4 %all-gather.5.cloned.1.call-done = bf16[1024,1536]{0,1:T(8,128)(2,1)} async-done(((bf16[1024,192]{0,1:T(8,128)(2,1)}), bf16[1024,1536]{0,1:T(8,128)(2,1)}) %all-gather.5.cloned.1.call-update) | async-done | bytes 3145744 | tf_op jit(solution)/shard_map/all_gather | solution.py:144
  200.1 8.0 %multiply_convert_fusion.1 = bf16[1024,768]{1,0:T(8,128)(2,1)S(1)} fusion(f32[1024,768]{1,0:T(8,128)} %copy-done.11, bf16[1024,1536]{0,1:T(8,128)(2,1)} %all-gather.5.cloned.1.call-done, bf16[1536,1536]{1,0:T(8,128)(2,1)} %all-gather.3.cloned.1.call-done), kind=kOutput, calls=%fused_computation.10 | convolution fusion | flops 2432434176 | bytes 10223616 | tf_op jit(solution)/shard_map/dot_general | solution.py:145
  208.0 2.8 convolution_multiply_fusion.1
  210.9 3.2 convolution_multiply_fusion
  214.1 4.5 %pad_maximum_fusion = f32[1536,1536]{0,1:T(8,128)} fusion(f32[1536,768]{0,1:T(8,128)S(1)} %convolution_multiply_fusion, f32[1536,768]{0,1:T(8,128)S(1)} %convolution_multiply_fusion.1), kind=kLoop, calls=%fused_computation | loop fusion | flops 2359296 | bytes 18874368 | tf_op jit(solution)/shard_map/concatenate | solution.py:31
  218.5 9.6 %copy.73 = f32[1536,1536]{1,0:T(8,128)} copy(f32[1536,1536]{0,1:T(8,128)} %pad_maximum_fusion) | data formatting | bytes 18874368
  228.2 101.6 %reduce-scatter.7.cloned.1.call-done = f32[48,1536]{1,0:T(8,128)} async-done(((f32[1536,1536]{1,0:T(8,128)}), f32[48,1536]{1,0:T(8,128)}) %reduce-scatter.7.cloned.1.call-update) | async-done | bytes 294928 | tf_op jit(solution)/shard_map/reduce_scatter | solution.py:33
  329.8 1.6 multiply_reduce_fusion.1
  332.7 9.9 %all-reduce.2 = (f32[]{:T(128)}, f32[]{:T(128)}) all-reduce(f32[]{:T(128)S(6)} %add.97, f32[]{:T(128)} %get-tuple-element.44), channel_id=1, replica_groups=mesh['dp_0'=4,'dp_1'=4,'dp_2'=2,'mp'=8] {'dp_0'}, use_global_device_ids=true, to_apply=%region_5.0 | all-reduce | flops 2 | bytes 16 | tf_op jit(solution)/shard_map/psum | solution.py:38
  342.6 10.1 %all-reduce.1 = (f32[]{:T(128)}, f32[]{:T(128)}) all-reduce(f32[]{:T(128)} %get-tuple-element.34, f32[]{:T(128)} %get-tuple-element.35), channel_id=1, replica_groups=mesh['dp_0'=4,'dp_1'=4,'dp_2'=2,'mp'=8] {'dp_1'}, use_global_device_ids=true, to_apply=%region_6.0 | all-reduce | flops 2 | bytes 16 | tf_op jit(solution)/shard_map/psum | solution.py:38
  352.7 3.1 all-reduce.3
  355.7 18.1 %all-reduce = (f32[]{:T(128)}, f32[]{:T(128)}) all-reduce(f32[]{:T(128)} %get-tuple-element.36, f32[]{:T(128)} %get-tuple-element.37), channel_id=1, replica_groups=mesh['dp_0'=4,'dp_1'=4,'dp_2'=2,'mp'=8] {'mp'}, use_global_device_ids=true, to_apply=%region_8.0 | all-reduce | flops 2 | bytes 16 | tf_op jit(solution)/shard_map/psum | solution.py:38
  375.2 2.0 multiply_subtract_fusion
  (38 shorter events, 0.7 us)
Async XLA Ops:
  7.2 89.3 %all-gather.3.cloned.1.call-start = ((), (), s32[]{:S(2)}) async-start(), calls=%async_computation.3 | async-start | bytes 4866048 | tf_op jit(solution)/shard_map/all_gather | solution.py:19
  9.8 140.9 %reduce-scatter.5.cloned.1.call-start = ((), (), s32[]{:S(2)}) async-start(), calls=%async_computation.4 | async-start | bytes 3538944 | tf_op jit(solution)/shard_map/reduce_scatter | solution.py:133
  96.4 6.2 %copy-start.9 = (bf16[1536,1536]{1,0:T(8,128)(2,1)S(1)}, bf16[1536,1536]{1,0:T(8,128)(2,1)}, u32[]{:S(2)}) copy-start(bf16[1536,1536]{1,0:T(8,128)(2,1)} %all-gather.3.cloned.1.call-done) | copy-start | bytes 14155780
  101.0 1.7 copy-start.11
  107.1 44.7 %copy-start = (bf16[4,256,192]{1,2,0:T(8,128)(2,1)S(1)}, bf16[4,256,192]{1,2,0:T(8,128)(2,1)}, u32[]{:S(2)}) copy-start(bf16[4,256,192]{1,2,0:T(8,128)(2,1)} %param.13) | copy-start | bytes 1179652
  107.2 92.9 %all-gather.5.cloned.1.call-start = ((), (), s32[]{:S(2)}) async-start(), calls=%async_computation.5 | async-start | bytes 3538944 | tf_op jit(solution)/shard_map/all_gather | solution.py:144
  107.9 1.2 copy-start.7
  150.7 3.8 copy-start.8
  155.5 174.3 %reduce-scatter.7.cloned.1.call-start = ((), (), s32[]{:S(2)}) async-start(), calls=%async_computation.6 | async-start | bytes 9732096 | tf_op jit(solution)/shard_map/reduce_scatter | solution.py:33
  208.0 2.8 copy-start.10
  208.0 2.8 copy-start.12
  228.2 147.0 %copy-start.1 = (f32[48,768]{1,0:T(8,128)S(1)}, f32[48,768]{1,0:T(8,128)}, u32[]{:S(2)}) copy-start(f32[48,768]{1,0:T(8,128)} %param.19) | copy-start | bytes 442372
  228.2 147.0 %copy-start.2 = (f32[48,768]{1,0:T(8,128)S(1)}, f32[48,768]{1,0:T(8,128)}, u32[]{:S(2)}) copy-start(f32[48,768]{1,0:T(8,128)} %param.18) | copy-start | bytes 442372
  228.2 147.0 %copy-start.3 = (f32[48,768]{1,0:T(8,128)S(1)}, f32[48,768]{1,0:T(8,128)}, u32[]{:S(2)}) copy-start(f32[48,768]{1,0:T(8,128)} %param.21) | copy-start | bytes 442372
  228.2 147.1 %copy-start.4 = (f32[48,768]{1,0:T(8,128)S(1)}, f32[48,768]{1,0:T(8,128)}, u32[]{:S(2)}) copy-start(f32[48,768]{1,0:T(8,128)} %param.23) | copy-start | bytes 442372
  228.2 147.1 %copy-start.5 = (f32[48,768]{1,0:T(8,128)S(1)}, f32[48,768]{1,0:T(8,128)}, u32[]{:S(2)}) copy-start(f32[48,768]{1,0:T(8,128)} %param.22) | copy-start | bytes 442372
  228.2 147.1 %copy-start.6 = (f32[48,768]{1,0:T(8,128)S(1)}, f32[48,768]{1,0:T(8,128)}, u32[]{:S(2)}) copy-start(f32[48,768]{1,0:T(8,128)} %param.20) | copy-start | bytes 442372
Sparse Core Ops, SparseCore 0:
  11.1 54.2 all-gather.2
  107.3 43.3 reduce-scatter.4
  155.6 44.4 all-gather.4
  228.3 101.4 reduce-scatter.6
